TPU v7x, 32 devices: a whole 2x2x4 slice. The times are simulated.
32 devices in a mesh: dp: 16 (over z, y, x), mp: 2 (over core).
Axes of the slice: x: 2, y: 2, z: 4, core: 2. Of those that a mesh axis runs over, the one named last changes fastest.
Arguments:
- pre_act: bfloat16 [8192, 16384], P('dp', 'mp'), may hold values from -8 to 8
- out_weight: bfloat16 [16384, 512], P('mp'), may hold values from -0.046875 to 0.046875
- out_grad: bfloat16 [8192, 512], P(('dp', 'mp')), may hold values from -2 to 2
Outputs:
- projected: bfloat16 [8192, 512], P(('dp', 'mp'))
- combined: float32 [16384, 512], P(('mp', 'dp'))
All inputs are finite; a program needn't handle non-finite values.
Results may differ from a plain program's by a relative error of at most 0.0005.
Values may be sent and summed in bfloat16 or wider, within the bound.
A program may use at most 128 MiB of HBM per device.

v0:
```python
import functools
import jax
import jax.numpy as jnp
from jax import lax
from jax.experimental import pallas as pl
from jax.experimental.pallas import tpu as pltpu
from jax.sharding import PartitionSpec as P

epsilon = 1e-06
MESH = pl.DeviceIdType.MESH


def from_partner(value, axis, apart):
    mask = 2**apart
    pairs = [(source, source ^ mask) for source in range(lax.axis_size(axis))]
    return lax.ppermute(value, axis, pairs)


def contract(left, right):
    return lax.dot_general(
        left, right, (((0,), (0,)), ((), ())), preferred_element_type=jnp.float32
    )


def split_rows(piece, block, which):
    width = piece.shape[1]
    blocks = piece.reshape(piece.shape[0] // (2 * block), 2, block, width)
    kept = lax.dynamic_index_in_dim(blocks, which, 1, False).reshape(-1, width)
    sent = lax.dynamic_index_in_dim(blocks, 1 - which, 1, False).reshape(-1, width)
    return (kept, sent)


def level_sums(partial_value, level):
    totals = lax.psum(partial_value, "mp")
    for inner_bit in range(level + 1):
        totals = totals + from_partner(totals, "dp", inner_bit)
    return totals


def merge_level(own, other, level, which):
    lower = which == 0
    own_sq = jnp.sum(own * own)
    other_sq = jnp.sum(other * other)
    partial_value = jnp.stack(
        [
            jnp.sum(own * other),
            jnp.where(lower, own_sq, other_sq),
            jnp.where(lower, other_sq, own_sq),
        ]
    )
    totals = level_sums(partial_value, level)
    first_coef = 1.0 - totals[0] / (2.0 * (totals[1] + epsilon))
    second_coef = 1.0 - totals[0] / (2.0 * (totals[2] + epsilon))
    own_coef = jnp.where(lower, first_coef, second_coef)
    other_coef = jnp.where(lower, second_coef, first_coef)
    return own_coef * own + other_coef * other


def halving(pre_act, out_weight, out_grad):
    act = jnp.maximum(pre_act, jnp.zeros((), jnp.bfloat16))
    tokens = act.shape[0]
    partial_out = jnp.dot(act, out_weight, preferred_element_type=jnp.float32)
    summed = lax.psum_scatter(partial_out, "mp", scatter_dimension=0, tiled=True)
    projected = summed.astype(jnp.bfloat16)
    grad_full = lax.all_gather(out_grad, "mp", axis=0, tiled=True)
    count = lax.axis_size("dp")
    levels = count.bit_length() - 1
    me = lax.axis_index("dp")
    block = act.shape[1] // count
    first_bit = me & 1
    groups = act.reshape(tokens, act.shape[1] // (2 * block), 2, block)
    kept_act = lax.dynamic_index_in_dim(groups, first_bit, 2, False).reshape(tokens, -1)
    sent_act = lax.dynamic_index_in_dim(groups, 1 - first_bit, 2, False).reshape(tokens, -1)
    packed = jnp.concatenate([sent_act, grad_full], axis=1)
    arrived = from_partner(packed, "dp", 0)
    half = sent_act.shape[1]
    own = contract(kept_act, grad_full)
    other = contract(arrived[:, :half], arrived[:, half:])
    piece = merge_level(own, other, 0, first_bit)
    for level in range(1, levels):
        which = me >> level & 1
        own, sent = split_rows(piece, block, which)
        other = from_partner(sent, "dp", level)
        piece = merge_level(own, other, level, which)
    return (projected, piece)


def put_lanes(values, rows):
    padded = -(-len(values) // 8) * 8
    strips = [jnp.sum(v, axis=0, keepdims=True) for v in values]
    strips += [jnp.zeros_like(strips[0])] * (padded - len(values))
    table = jnp.concatenate(strips, axis=0)
    totals = jnp.sum(table, axis=1, keepdims=True)
    lane = lax.broadcasted_iota(jnp.int32, table.shape, 1)
    row = lax.broadcasted_iota(jnp.int32, table.shape, 0)
    line = jnp.sum(jnp.where(lane == row, totals, 0.0), axis=0, keepdims=True)
    return jnp.broadcast_to(line, (rows, line.shape[1]))


def lane_value(line, p):
    lane = lax.broadcasted_iota(jnp.int32, line.shape, 1)
    return jnp.sum(jnp.where(lane == p, line, 0.0), axis=1, keepdims=True)


def kernel(
    n_dp, pre, w, og, proj, comb,
    acts, grads_in, leaf, node, arrived, xbuf, wbuf, acc, part_in, slots, slots3,
    act_send, act_recv, og_send, og_recv, mate_send, mate_recv, local_sem, own_sem,
    fwd_sem, part_sem, slot_send, slot_recv, node_send, node_recv, slot3_send, slot3_recv,
):
    dp = lax.axis_index("dp")
    core = lax.axis_index("mp")
    group = n_dp // 2
    bits = group.bit_length() - 1
    me = lax.rem(dp, group)
    high = dp // group
    base = high * group
    tokens = pre.shape[0]
    block = pre.shape[1] // n_dp
    own_rows = og.shape[0]
    width = og.shape[1]
    mate = 1 - core
    me_bits = [lax.rem(me // 2**b, 2) for b in range(bits)]

    def flip(r):
        total = 0
        for b in range(bits):
            rb = (r // 2**b) % 2 if isinstance(r, int) else lax.rem(r // 2**b, 2)
            total = total + 2**b * (me_bits[b] + rb - 2 * me_bits[b] * rb)
        return total

    barrier = pltpu.get_barrier_semaphore()
    for q in range(1, 2 * n_dp):
        other = lax.rem(dp * 2 + core + q, 2 * n_dp)
        pl.semaphore_signal(
            barrier, inc=1, device_id=(other // 2, lax.rem(other, 2)), device_id_type=MESH
        )

    my_og = grads_in.at[me, pl.ds(core * own_rows, own_rows)]
    og_local = pltpu.make_async_copy(og, my_og, local_sem)
    og_local.start()

    def own_copy(h):
        cols = pl.ds(pl.multiple_of((me + group * h) * block, block), block)
        return pltpu.make_async_copy(pre.at[:, cols], acts.at[me, h], own_sem.at[h])

    own_copy(0).start()
    own_copy(1).start()
    og_local.wait()
    pl.semaphore_wait(barrier, 2 * n_dp - 1)

    def og_copy(r):
        at, to = flip(RELAY[r][0]), flip(RELAY[r][1])
        rows = grads_in.at[at, pl.ds(core * own_rows, own_rows)]
        return pltpu.make_async_remote_copy(
            src_ref=rows, dst_ref=rows, send_sem=og_send.at[r], recv_sem=og_recv.at[r],
            device_id=(base + to, core), device_id_type=MESH,
        )

    def og_arrival(r):
        rows = grads_in.at[flip(r), pl.ds(core * own_rows, own_rows)]
        pltpu.make_async_remote_copy(
            src_ref=rows, dst_ref=rows, send_sem=og_send.at[r], recv_sem=og_recv.at[r],
            device_id=(base + flip(r), core), device_id_type=MESH,
        ).wait_recv()
        mate_copy(r, flip(r), core).start()

    def act_copy(r, i, h, at):
        cols = pl.ds(pl.multiple_of((i + group * h) * block, block), block)
        return pltpu.make_async_remote_copy(
            src_ref=pre.at[:, cols], dst_ref=acts.at[at, h],
            send_sem=act_send.at[r, h], recv_sem=act_recv.at[r, h],
            device_id=(base + i, core), device_id_type=MESH,
        )

    def mate_copy(r, i, side):
        rows = grads_in.at[i, pl.ds(side * own_rows, own_rows)]
        return pltpu.make_async_remote_copy(
            src_ref=rows, dst_ref=rows, send_sem=mate_send.at[r], recv_sem=mate_recv.at[r],
            device_id=(dp, mate), device_id_type=MESH,
        )

    mate_copy(0, me, core).start()
    for r in (4, 1, 2):
        og_copy(r).start()
    act_copy(7, flip(7), 0, me).start()
    og_arrival(2)
    og_copy(6).start()
    for h in range(2):
        for lead, _ in SLOTS:
            if (lead, h) != (7, 0):
                act_copy(lead, flip(lead), h, me).start()
    og_arrival(4)
    og_copy(5).start()
    og_arrival(1)
    og_copy(3).start()
    for h in range(2):
        for r in (2, 1, 3):
            act_copy(r, flip(r), h, me).start()

    step_cols = xbuf.shape[2]
    steps = pre.shape[1] // step_cols

    def fetch(k, slot):
        cols = pl.ds(pl.multiple_of(k * step_cols, step_cols), step_cols)
        return (
            pltpu.make_async_copy(pre.at[:, cols], xbuf.at[slot], fwd_sem.at[slot, 0]),
            pltpu.make_async_copy(w.at[cols, :], wbuf.at[slot], fwd_sem.at[slot, 1]),
        )

    for c in fetch(0, 0):
        c.start()
    acc[...] = jnp.zeros_like(acc)

    def forward(k, carry):
        slot = lax.rem(k, 2)

        @pl.when(k + 1 < steps)
        def _():
            for c in fetch(k + 1, 1 - slot):
                c.start()

        for c in fetch(k, slot):
            c.wait()
        x = jnp.maximum(xbuf[slot], jnp.zeros((), jnp.bfloat16))
        acc[...] += jnp.dot(x, wbuf[slot], preferred_element_type=jnp.float32)
        return carry

    lax.fori_loop(0, steps, forward, 0)
    part = pltpu.make_async_remote_copy(
        src_ref=acc.at[pl.ds(mate * own_rows, own_rows)], dst_ref=part_in,
        send_sem=part_sem.at[0], recv_sem=part_sem.at[1],
        device_id=(dp, mate), device_id_type=MESH,
    )
    part.start()

    og_arrival(6)
    og_copy(7).start()
    for r in (5, 3, 7):
        og_arrival(r)
    part.wait_recv()
    proj[...] = (acc[pl.ds(core * own_rows, own_rows), :] + part_in[...]).astype(proj.dtype)
    for r in range(group):
        mate_copy(r, flip(r), mate).wait_recv()

    pairs = [(i, j) for i in range(group) for j in range(i, group)]
    sums = tuple(jnp.zeros((8, 128), jnp.float32) for _ in pairs)
    def gram_rows(h, sums):
        def gram(t, carry):
            rows = pl.ds(pl.multiple_of(h * block + t * 8, 8), 8)
            for c in range(width // 128):
                v = [leaf[i, rows, c * 128:(c + 1) * 128] for i in range(group)]
                carry = tuple(s + v[i] * v[j] for s, (i, j) in zip(carry, pairs))
            return carry

        return lax.fori_loop(0, block // 8, gram, sums)

    for h in range(2):
        def leaf_grad(i):
            a = jnp.maximum(acts[i, h], jnp.zeros((), jnp.bfloat16))
            leaf[i, pl.ds(h * block, block), :] = contract(a, grads_in[i])

        own_copy(h).wait()
        leaf_grad(me)
        for n, (lead, beside) in enumerate(SLOTS):
            act_copy(lead, flip(lead), h, me).wait_send()
            if h == 1 and n == 0:
                sums = gram_rows(0, sums)
            for r in (lead, beside):
                if r:
                    i = flip(r)
                    act_copy(r, i, h, i).wait_recv()
                    leaf_grad(i)

        if h == 1:
            sums = gram_rows(1, sums)

    mine = me * 2 + core
    slots[mine] = put_lanes(list(sums), 8)

    def slot_copy(q, other, at):
        return pltpu.make_async_remote_copy(
            src_ref=slots.at[at], dst_ref=slots.at[at],
            send_sem=slot_send.at[q], recv_sem=slot_recv.at[at],
            device_id=(base + other // 2, lax.rem(other, 2)), device_id_type=MESH,
        )

    for q in range(1, 2 * group):
        slot_copy(q, lax.rem(mine + q, 2 * group), mine).start()
    for q in range(1, 2 * group):
        other = lax.rem(mine + q, 2 * group)
        slot_copy(q, other, other).wait_recv()
    line = slots[0]
    for k in range(1, 2 * group):
        line = line + slots[k]
    line = line[0:1]
    table = {}
    for p, (i, j) in enumerate(pairs):
        table[i, j] = table[j, i] = lane_value(line, p)
    coef = [jnp.ones((1, 1), jnp.float32) for _ in range(group)]

    def form(left, right):
        total = jnp.zeros((1, 1), jnp.float32)
        for i in left:
            for j in right:
                total = total + coef[i] * coef[j] * table[i, j]
        return total

    for level in range(bits):
        size = 2**level
        fresh = list(coef)
        for start in range(0, group, 2 * size):
            left = range(start, start + size)
            right = range(start + size, start + 2 * size)
            s = form(left, right)
            first = 1.0 - s / (2.0 * (jnp.maximum(form(left, left), 0.0) + epsilon))
            second = 1.0 - s / (2.0 * (jnp.maximum(form(right, right), 0.0) + epsilon))
            for i in left:
                fresh[i] = coef[i] * first
            for j in right:
                fresh[j] = coef[j] * second
        coef = fresh

    wide = [jnp.broadcast_to(c, (8, width)) for c in coef]

    def build(h):
        def strip(t, carry):
            rows = pl.ds(pl.multiple_of(h * block + t * 8, 8), 8)
            total = wide[0] * leaf[0, rows, :]
            for i in range(1, group):
                total = total + wide[i] * leaf[i, rows, :]
            node[h, pl.ds(pl.multiple_of(t * 8, 8), 8), :] = total
            return carry
        lax.fori_loop(0, block // 8, strip, 0)

    far = lax.rem(dp + group, n_dp)
    pieces = node_send.shape[0]
    tall = block // pieces

    def node_copy(k):
        rows = pl.ds(k * tall, tall)
        return pltpu.make_async_remote_copy(
            src_ref=node.at[1 - high, rows], dst_ref=arrived.at[rows],
            send_sem=node_send.at[k], recv_sem=node_recv.at[k],
            device_id=(far, core), device_id_type=MESH,
        )

    build(1 - high)
    for k in range(pieces):
        node_copy(k).start()
    build(high)

    sums = tuple(jnp.zeros((8, 128), jnp.float32) for _ in range(3))
    for k in range(pieces):
        node_copy(k).wait_recv()

        def inner(t, carry):
            rows = pl.ds(pl.multiple_of(k * tall + t * 8, 8), 8)
            s, q, r = carry
            for c in range(width // 128):
                a = node[high, rows, c * 128:(c + 1) * 128]
                b = arrived[rows, c * 128:(c + 1) * 128]
                s, q, r = s + a * b, q + a * a, r + b * b
            return s, q, r

        sums = lax.fori_loop(0, tall // 8, inner, sums)
    up = high.astype(jnp.float32)
    low_sq = (1.0 - up) * sums[1] + up * sums[2]
    high_sq = up * sums[1] + (1.0 - up) * sums[2]
    place = dp * 2 + core
    slots3[place] = put_lanes([sums[0], low_sq, high_sq], 8)

    def slot3_copy(q, other, at):
        return pltpu.make_async_remote_copy(
            src_ref=slots3.at[at], dst_ref=slots3.at[at],
            send_sem=slot3_send.at[q], recv_sem=slot3_recv.at[at],
            device_id=(other // 2, lax.rem(other, 2)), device_id_type=MESH,
        )

    for q in range(1, 2 * n_dp):
        slot3_copy(q, lax.rem(place + q, 2 * n_dp), place).start()
    for q in range(1, 2 * n_dp):
        other = lax.rem(place + q, 2 * n_dp)
        slot3_copy(q, other, other).wait_recv()
    line = slots3[0]
    for k in range(1, 2 * n_dp):
        line = line + slots3[k]
    line = line[0:1]
    s = lane_value(line, 0)
    low = 1.0 - s / (2.0 * (lane_value(line, 1) + epsilon))
    top = 1.0 - s / (2.0 * (lane_value(line, 2) + epsilon))
    own_coef = jnp.broadcast_to((1.0 - up) * low + up * top, (8, width))
    far_coef = jnp.broadcast_to(up * low + (1.0 - up) * top, (8, width))

    def last(t, carry):
        rows = pl.ds(pl.multiple_of(t * 8, 8), 8)
        comb[rows, :] = own_coef * node[high, rows, :] + far_coef * arrived[rows, :]
        return carry

    lax.fori_loop(0, block // 8, last, 0)

    mate_copy(0, me, core).wait_send()
    for r in range(1, group):
        i = flip(r)
        og_copy(r).wait_send()
        mate_copy(r, i, core).wait_send()
    for _, r in SLOTS:
        if r:
            for h in range(2):
                act_copy(r, flip(r), h, me).wait_send()
    part.wait_send()
    for q in range(1, 2 * group):
        slot_copy(q, lax.rem(mine + q, 2 * group), mine).wait_send()
    for k in range(pieces):
        node_copy(k).wait_send()
    for q in range(1, 2 * n_dp):
        slot3_copy(q, lax.rem(place + q, 2 * n_dp), place).wait_send()


SLOTS = ((7, 0), (5, 2), (6, 1), (4, 3))
RELAY = {1: (0, 1), 2: (0, 2), 4: (0, 4), 3: (1, 2), 6: (2, 4), 5: (4, 1), 7: (6, 1)}


def exchange(n_dp, pre_act, out_weight, out_grad):
    tokens, hidden = pre_act.shape
    block = hidden // n_dp
    group = n_dp // 2
    width = out_grad.shape[1]
    own_rows = out_grad.shape[0]
    step_cols = hidden // 8
    pieces = 4
    dma = pltpu.SemaphoreType.DMA
    hbm = pl.BlockSpec(memory_space=pl.ANY)
    vmem = pl.BlockSpec(memory_space=pltpu.VMEM)
    return pl.pallas_call(
        functools.partial(kernel, n_dp),
        out_shape=(
            jax.ShapeDtypeStruct((own_rows, width), jnp.bfloat16),
            jax.ShapeDtypeStruct((block, width), jnp.float32),
        ),
        in_specs=[hbm, hbm, hbm],
        out_specs=(vmem, vmem),
        scratch_shapes=[
            pltpu.VMEM((group, 2, tokens, block), jnp.bfloat16),
            pltpu.VMEM((group, tokens, width), jnp.bfloat16),
            pltpu.VMEM((group, 2 * block, width), jnp.float32),
            pltpu.VMEM((2, block, width), jnp.float32),
            pltpu.VMEM((block, width), jnp.float32),
            pltpu.VMEM((2, tokens, step_cols), jnp.bfloat16),
            pltpu.VMEM((2, step_cols, width), jnp.bfloat16),
            pltpu.VMEM((tokens, width), jnp.float32),
            pltpu.VMEM((own_rows, width), jnp.float32),
            pltpu.VMEM((2 * group, 8, 128), jnp.float32),
            pltpu.VMEM((2 * n_dp, 8, 128), jnp.float32),
            dma((group, 2)), dma((group, 2)), dma((group,)), dma((group,)),
            dma((group,)), dma((group,)), dma, dma((2,)),
            dma((2, 2)), dma((2,)), dma((2 * group,)), dma((2 * group,)),
            dma((pieces,)), dma((pieces,)), dma((2 * n_dp,)), dma((2 * n_dp,)),
        ],
        compiler_params=pltpu.CompilerParams(
            collective_id=0, has_side_effects=True, vmem_limit_bytes=60 * 2**20
        ),
    )(pre_act, out_weight, out_grad)


def local(pre_act, out_weight, out_grad):
    n_dp = lax.axis_size("dp")
    block = pre_act.shape[1] // n_dp
    rows = out_grad.shape[0]
    if lax.axis_size("mp") == 2 and n_dp == 4 * len(SLOTS) and block % 128 == 0 and rows % 16 == 0:
        return exchange(n_dp, pre_act, out_weight, out_grad)
    return halving(pre_act, out_weight, out_grad)


def solution(mesh):
    placed = (P("dp", "mp"), P("mp", None), P(("dp", "mp"), None))
    return jax.shard_map(
        local,
        mesh=mesh,
        in_specs=placed,
        out_specs=(P(("dp", "mp"), None), P(("mp", "dp"), None)),
        check_vma=False,
    )
```

profile of v0, /device:TPU:0, one launch (start us, length us, event | category | flops | bytes accessed | tf_op | source)
XLA Modules:
  0.0 196.5 jit_solution(13596292255640004105)
XLA Ops:
  0.6 191.9 %shard_map.50 = (bf16[256,512]{1,0:T(8,128)(2,1)}, f32[512,512]{1,0:T(8,128)}) custom-call(bf16[512,8192]{1,0:T(8,128)(2,1)} %pre.1, bf16[8192,512]{1,0:T(8,128)(2,1)} %w.1, bf16[256,512]{1,0:T(8,128)(2,1)} %og.1), custom_call_target="tpu_custom_call" | custom-call | tf_op jit(solution)/shard_map/pallas_call | solution.py:435
  192.6 1.7 copy.7
  194.2 2.3 %copy.8 = f32[512,512]{1,0:T(8,128)} copy(f32[512,512]{1,0:T(8,128)} %get-tuple-element.5) | data formatting | bytes 2097152
where the time goes:
time: 197 us
  Pallas kernels  192 us (97%)
  local copies, waits for them, and re-layouts  3.93 us (2%)
    pallas_call x1, Pallas kernels, exchange(): pl.pallas_call(functools.partial(kernel, n_dp), out_shape=(jax.ShapeDtype...  192 us

commit v1 on v0

v1 whole, which is shorter than its diff:
```python
import functools
import jax
import jax.numpy as jnp
from jax import lax
from jax.experimental import pallas as pl
from jax.experimental.pallas import tpu as pltpu
from jax.sharding import PartitionSpec as P

epsilon = 1e-06
MESH = pl.DeviceIdType.MESH


def from_partner(value, axis, apart):
    mask = 2**apart
    pairs = [(source, source ^ mask) for source in range(lax.axis_size(axis))]
    return lax.ppermute(value, axis, pairs)


def contract(left, right):
    return lax.dot_general(
        left, right, (((0,), (0,)), ((), ())), preferred_element_type=jnp.float32
    )


def split_rows(piece, block, which):
    width = piece.shape[1]
    blocks = piece.reshape(piece.shape[0] // (2 * block), 2, block, width)
    kept = lax.dynamic_index_in_dim(blocks, which, 1, False).reshape(-1, width)
    sent = lax.dynamic_index_in_dim(blocks, 1 - which, 1, False).reshape(-1, width)
    return (kept, sent)


def level_sums(partial_value, level):
    totals = lax.psum(partial_value, "mp")
    for inner_bit in range(level + 1):
        totals = totals + from_partner(totals, "dp", inner_bit)
    return totals


def merge_level(own, other, level, which):
    lower = which == 0
    own_sq = jnp.sum(own * own)
    other_sq = jnp.sum(other * other)
    partial_value = jnp.stack(
        [
            jnp.sum(own * other),
            jnp.where(lower, own_sq, other_sq),
            jnp.where(lower, other_sq, own_sq),
        ]
    )
    totals = level_sums(partial_value, level)
    first_coef = 1.0 - totals[0] / (2.0 * (totals[1] + epsilon))
    second_coef = 1.0 - totals[0] / (2.0 * (totals[2] + epsilon))
    own_coef = jnp.where(lower, first_coef, second_coef)
    other_coef = jnp.where(lower, second_coef, first_coef)
    return own_coef * own + other_coef * other


def halving(pre_act, out_weight, out_grad):
    act = jnp.maximum(pre_act, jnp.zeros((), jnp.bfloat16))
    tokens = act.shape[0]
    partial_out = jnp.dot(act, out_weight, preferred_element_type=jnp.float32)
    summed = lax.psum_scatter(partial_out, "mp", scatter_dimension=0, tiled=True)
    projected = summed.astype(jnp.bfloat16)
    grad_full = lax.all_gather(out_grad, "mp", axis=0, tiled=True)
    count = lax.axis_size("dp")
    levels = count.bit_length() - 1
    me = lax.axis_index("dp")
    block = act.shape[1] // count
    first_bit = me & 1
    groups = act.reshape(tokens, act.shape[1] // (2 * block), 2, block)
    kept_act = lax.dynamic_index_in_dim(groups, first_bit, 2, False).reshape(tokens, -1)
    sent_act = lax.dynamic_index_in_dim(groups, 1 - first_bit, 2, False).reshape(tokens, -1)
    packed = jnp.concatenate([sent_act, grad_full], axis=1)
    arrived = from_partner(packed, "dp", 0)
    half = sent_act.shape[1]
    own = contract(kept_act, grad_full)
    other = contract(arrived[:, :half], arrived[:, half:])
    piece = merge_level(own, other, 0, first_bit)
    for level in range(1, levels):
        which = me >> level & 1
        own, sent = split_rows(piece, block, which)
        other = from_partner(sent, "dp", level)
        piece = merge_level(own, other, level, which)
    return (projected, piece)


def row_of(values):
    parts = [jnp.sum(v, axis=0, keepdims=True) for v in values]
    parts += [jnp.zeros_like(parts[0])] * (8 - len(parts))
    table = jnp.concatenate(parts, axis=0)
    return line_of(table)


def line_of(table):
    totals = jnp.sum(table, axis=1, keepdims=True)
    lane = lax.broadcasted_iota(jnp.int32, table.shape, 1)
    row = lax.broadcasted_iota(jnp.int32, table.shape, 0)
    return jnp.sum(jnp.where(lane == row, totals, 0.0), axis=0, keepdims=True)


def lane_value(line, p):
    lane = lax.broadcasted_iota(jnp.int32, line.shape, 1)
    return jnp.sum(jnp.where(lane == p, line, 0.0), axis=1, keepdims=True)


def swap(value, axis, bit):
    size = value.shape[axis]
    at = lax.broadcasted_iota(jnp.int32, value.shape, axis)
    up = pltpu.roll(value, size - bit, axis)
    down = pltpu.roll(value, bit, axis)
    return jnp.where((at // bit) % 2 == 0, up, down)


def tree_coefs(line, group):
    rows = 2 * group
    lanes = line.shape[1]
    m = jnp.concatenate([pltpu.roll(jnp.broadcast_to(line, (8, lanes)), group * r, 1)[0:1] if r else line for r in range(rows)], axis=0)
    lane = lax.broadcasted_iota(jnp.int32, m.shape, 1)
    own = lax.broadcasted_iota(jnp.int32, m.shape, 0) % group
    coef = jnp.ones_like(m)
    for level in range(group.bit_length() - 1):
        bit = 2**level
        mate = jnp.where((own // bit) % 2 == 0, own + bit, own - bit)
        inner = jnp.sum(jnp.where(lane == mate, m, 0.0), axis=1, keepdims=True)
        square = jnp.sum(jnp.where(lane == own, m, 0.0), axis=1, keepdims=True)
        f = 1.0 - inner / (2.0 * (jnp.maximum(square, 0.0) + epsilon))
        f = jnp.broadcast_to(f, m.shape)
        coef = coef * f
        across = jnp.where(lane == own, f, 0.0)
        across = jnp.concatenate(
            [jnp.broadcast_to(jnp.sum(across[g * group:(g + 1) * group], axis=0, keepdims=True), (group, lanes)) for g in range(2)],
            axis=0,
        )
        m = m * f * across
        m = m + swap(m, 1, bit)
        m = m + swap(m, 0, bit)
    return coef


def kernel(
    n_dp, pre, w, og, proj, comb,
    acts, grads, leaf, node, arrived, xbuf, wbuf, acc, part_in, gsum, slots, slots3, coefs,
    act_send, act_recv, og_send, og_recv, mate_send, mate_recv, local_sem,
    fwd_sem, part_sem, slot_send, slot_recv, node_send, node_recv, slot3_send, slot3_recv,
):
    dp = lax.axis_index("dp")
    core = lax.axis_index("mp")
    group = n_dp // 2
    me = lax.rem(dp, group)
    z = dp // 4
    y = lax.rem(dp // 2, 2)
    x = lax.rem(dp, 2)
    high = z // 2
    zi = 2 * high + 1 - lax.rem(z, 2)
    tokens = pre.shape[0]
    block = pre.shape[1] // n_dp
    own_rows = og.shape[0]
    width = og.shape[1]
    mate = 1 - core
    edge_z, mid_z = 3 * high, 1 + high
    far_edge_z, far_mid_z = 3 - 3 * high, 2 - high
    edge = z == edge_z
    mid = z == mid_z

    def spot(at_z, m):
        dx = lax.rem(m, 2) if not isinstance(m, int) else m % 2
        dy = m // 2
        return at_z * 4 + (y + dy - 2 * dy * y) * 2 + x + dx - 2 * dx * x

    def turn(j):
        k = core * (ORDER[(j + 2) % 4] - ORDER[j]) + ORDER[j]
        return k

    barrier = pltpu.get_barrier_semaphore()
    for q in range(1, 2 * n_dp):
        other = lax.rem(dp * 2 + core + q, 2 * n_dp)
        pl.semaphore_signal(
            barrier, inc=1, device_id=(other // 2, lax.rem(other, 2)), device_id_type=MESH
        )

    def half(i, side):
        return grads.at[i, pl.ds(side * own_rows, own_rows)]

    og_local = pltpu.make_async_copy(og, half(dp, core), local_sem)
    og_local.start()

    def cols(b):
        return pl.ds(pl.multiple_of(b * block, block), block)

    def self_copy(b, slot):
        return pltpu.make_async_copy(pre.at[:, cols(b)], acts.at[slot], act_recv.at[slot])

    step_cols = xbuf.shape[2]
    steps = pre.shape[1] // step_cols

    def fetch(k, slot):
        here = pl.ds(pl.multiple_of(k * step_cols, step_cols), step_cols)
        return (
            pltpu.make_async_copy(pre.at[:, here], xbuf.at[slot], fwd_sem.at[slot, 0]),
            pltpu.make_async_copy(w.at[here, :], wbuf.at[slot], fwd_sem.at[slot, 1]),
        )

    for c in fetch(0, 0):
        c.start()
    acc[...] = jnp.zeros_like(acc)
    gsum[...] = jnp.zeros_like(gsum)

    def og_copy(n, i, to):
        return pltpu.make_async_remote_copy(
            src_ref=half(i, core), dst_ref=half(i, core), send_sem=og_send.at[n],
            recv_sem=og_recv.at[i], device_id=(to, core), device_id_type=MESH,
        )

    def mate_copy(i, side):
        return pltpu.make_async_remote_copy(
            src_ref=half(i, side), dst_ref=half(i, side), send_sem=mate_send.at[i],
            recv_sem=mate_recv.at[i], device_id=(dp, mate), device_id_type=MESH,
        )

    def og_arrival(i):
        og_copy(0, i, dp).wait_recv()
        mate_copy(i, core).start()

    def act_copy(kind, m):
        if kind < 2:
            to = spot(edge_z, m)
            b, slot = (to if kind == 0 else spot(far_edge_z, m)), me * 2 + kind
        else:
            to = spot(mid_z if kind == 2 else far_mid_z, m)
            b, slot = to, dp
        return pltpu.make_async_remote_copy(
            src_ref=pre.at[:, cols(b)], dst_ref=acts.at[slot],
            send_sem=act_send.at[kind * 4 + m], recv_sem=act_recv.at[slot],
            device_id=(to, core), device_id_type=MESH,
        )

    def plan(batch, where):
        return [(kind, turn(m - 4) if m > 3 else m) for kind, m in BATCHES[where][batch]]

    def send_acts(batch):
        for where, here in ((0, edge), (1, mid)):
            @pl.when(here)
            def _():
                for kind, m in plan(batch, where):
                    act_copy(kind, m).start()

    og_local.wait()
    pl.semaphore_wait(barrier, 2 * n_dp - 1)

    cross, along = 2 - core, 1 + core
    common = (
        ((z, 0, z, 1), (z, 0, z, 2), (z, 0, zi, 0)),
        ((z, cross, z, along), (z, 1, zi, 0), (z, 2, zi, 0)),
        ((z, 3, zi, 0),),
        (),
    )
    extra = (
        ((z, 0, far_mid_z, 0),),
        ((zi, 0, far_mid_z, 0), (far_mid_z, 0, z, 1), (far_mid_z, 0, z, 2)),
        ((z, 3, far_mid_z, 0), (far_edge_z, 0, z, 1), (far_edge_z, 0, z, 2)),
        ((far_edge_z, cross, z, along),),
    )
    landed = (
        ((), ()),
        (((z, 1), (z, 2), (zi, 0)), ((far_mid_z, 0),)),
        (((z, 3), (zi, 1), (zi, 2)), ((far_edge_z, 0), (far_mid_z, 1), (far_mid_z, 2))),
        (((zi, 3),), ((far_mid_z, 3), (far_edge_z, 1), (far_edge_z, 2))),
        ((), ((far_edge_z, 3),)),
    )

    def og_wave(k, moves):
        base = sum(len(c) for c in moves[:k])
        base += sum(len(c) for c in common) if moves is extra else 0
        return [og_copy(base + n, spot(a, m), spot(b, r)) for n, (a, m, b, r) in enumerate(moves[k])]

    def wave(k):
        for i in landed[k][0]:
            og_arrival(spot(*i))

        @pl.when(mid)
        def _():
            for i in landed[k][1]:
                og_arrival(spot(*i))

        if k < len(common):
            for c in og_wave(k, common):
                c.start()

            @pl.when(mid)
            def _():
                for c in og_wave(k, extra):
                    c.start()

            send_acts(k)

    wave(0)
    mate_copy(dp, core).start()

    @pl.when(edge)
    def _():
        self_copy(dp, me * 2).start()
        self_copy(spot(far_edge_z, 0), me * 2 + 1).start()

    @pl.when(mid)
    def _():
        self_copy(dp, dp).start()

    def forward(k, carry):
        slot = lax.rem(k, 2)

        @pl.when(k + 1 < steps)
        def _():
            for c in fetch(k + 1, 1 - slot):
                c.start()

        for c in fetch(k, slot):
            c.wait()
        v = jnp.maximum(xbuf[slot], jnp.zeros((), jnp.bfloat16))
        acc[...] += jnp.dot(v, wbuf[slot], preferred_element_type=jnp.float32)
        return carry

    lax.fori_loop(0, steps, forward, 0)
    part = pltpu.make_async_remote_copy(
        src_ref=acc.at[pl.ds(mate * own_rows, own_rows)], dst_ref=part_in,
        send_sem=part_sem.at[0], recv_sem=part_sem.at[1],
        device_id=(dp, mate), device_id_type=MESH,
    )
    part.start()
    wave(1)
    part.wait_recv()
    proj[...] = (acc[pl.ds(core * own_rows, own_rows), :] + part_in[...]).astype(proj.dtype)
    wave(2)
    wave(3)
    wave(4)

    def settle(i):
        mate_copy(i, mate).wait_recv()

    def leaf_grad(i, slot, own):
        if own:
            self_copy(0, slot).wait()
        else:
            pltpu.make_async_remote_copy(
                src_ref=pre.at[:, cols(0)], dst_ref=acts.at[slot], send_sem=act_send.at[0],
                recv_sem=act_recv.at[slot], device_id=(dp, mate), device_id_type=MESH,
            ).wait_recv()
        a = jnp.maximum(acts[slot], jnp.zeros((), jnp.bfloat16))
        leaf[slot] = contract(a, grads[i])

    def gram(new, others):
        i, slot = new
        seen = others + [new]

        def strip(t, carry):
            rows = pl.ds(pl.multiple_of(t * 8, 8), 8)
            for c in range(width // 128):
                lanes = slice(c * 128, (c + 1) * 128)
                v = leaf[slot, rows, lanes]
                carry = tuple(s + v * leaf[o, rows, lanes] for s, (_, o) in zip(carry, seen[:-1])) + (carry[-1] + v * v,)
            return carry

        zero = jnp.zeros((8, 128), jnp.float32)
        sums = lax.fori_loop(0, block // 8, strip, (zero,) * len(seen))
        for s, (j, _) in zip(sums, seen):
            line = jnp.sum(s, axis=0, keepdims=True)
            for p, q in ((i, j), (j, i))[: 1 if j is i else 2]:
                at = pl.ds(lax.rem(2 * group - p, 2 * group) * group + lax.rem(q, group), 1)
                gsum[at, :] += line

    @pl.when(edge)
    def _():
        def both(h, carry):
            done = []
            for n, (at_z, m) in enumerate([(z, 0), (z, 3), (z, 2), (z, 1)] + [(zi, turn(j)) for j in range(4)]):
                i = spot(at_z, m)

                @pl.when(h == 0)
                def _():
                    settle(i)

                slot = lax.rem(i, group) * 2 + h
                leaf_grad(i, slot, n == 0)
                gram((i, slot), done)
                done = done + [(i, slot)]
            return carry

        lax.fori_loop(0, 2, both, 0)

    @pl.when(mid)
    def _():
        near, away = [], []

        def take(i, seen):
            settle(i)
            leaf_grad(i, i, i is home)
            gram((i, i), seen)
            seen.append((i, i))

        home = spot(z, 0)
        take(home, near)
        for m in (3, 2, 1):
            take(spot(z, m), near)
        for j in range(4):
            take(spot(far_edge_z, turn(j)), away)
        for j in range(4):
            take(spot(far_mid_z, turn(j)), away)
            take(spot(zi, turn(j)), near)

    def gather(buf, send, recv, line):
        mine = dp * 2 + core
        buf[mine] = line

        def copy(q, other, at):
            return pltpu.make_async_remote_copy(
                src_ref=buf.at[at], dst_ref=buf.at[at], send_sem=send.at[q], recv_sem=recv.at[at],
                device_id=(other // 2, lax.rem(other, 2)), device_id_type=MESH,
            )

        def go(q, carry):
            copy(q, lax.rem(mine + q, 2 * n_dp), mine).start()
            return carry

        def take(q, carry):
            other = lax.rem(mine + q, 2 * n_dp)
            copy(q, other, other).wait_recv()
            return carry

        def left(q, carry):
            copy(q, lax.rem(mine + q, 2 * n_dp), mine).wait_send()
            return carry

        def finish():
            lax.fori_loop(1, 2 * n_dp, take, 0)
            total = buf[0]
            for k in range(1, 2 * n_dp):
                total = total + buf[k]
            return total

        lax.fori_loop(1, 2 * n_dp, go, 0)
        return finish, lambda: lax.fori_loop(1, 2 * n_dp, left, 0)

    finish, sent = gather(slots, slot_send, slot_recv, line_of(gsum[...]))
    coefs[...] = tree_coefs(finish(), group)

    def weights(first):
        return [jnp.broadcast_to(coefs[pl.ds(first + k, 1), :], (8, 128)) for k in range(group)]

    pieces = node_send.shape[0]
    tall = block // pieces

    def mix(weight, places, rows, lanes):
        total = weight[0] * leaf[places[0], rows, lanes]
        for k in range(1, group):
            total = total + weight[k] * leaf[places[k], rows, lanes]
        return total

    zero = jnp.zeros((8, 128), jnp.float32)
    far = spot(far_edge_z, 0)

    def node_copy(k):
        rows = pl.ds(k * tall, tall)
        return pltpu.make_async_remote_copy(
            src_ref=node.at[1, rows], dst_ref=arrived.at[rows],
            send_sem=node_send.at[k], recv_sem=node_recv.at[k],
            device_id=(far, core), device_id_type=MESH,
        )

    sums3 = slots3.at[dp * 2 + core]
    up = high.astype(jnp.float32)

    @pl.when(edge)
    def _():
        weight = weights(high * group)

        def build(h, first, count, q):
            def strip(t, q):
                rows = pl.ds(pl.multiple_of(first + t * 8, 8), 8)
                for c in range(width // 128):
                    lanes = slice(c * 128, (c + 1) * 128)
                    total = mix(weight, [2 * k + h for k in range(group)], rows, lanes)
                    node[h, rows, lanes] = total
                    q = q + total * total
                return q
            return lax.fori_loop(0, count // 8, strip, q)

        q = zero
        for k in range(pieces):
            q = build(1, k * tall, tall, q)
            node_copy(k).start()
        q = build(0, 0, block, q)
        s = zero
        for k in range(pieces):
            node_copy(k).wait_recv()

            def inner(t, s):
                rows = pl.ds(pl.multiple_of(k * tall + t * 8, 8), 8)
                for c in range(width // 128):
                    lanes = slice(c * 128, (c + 1) * 128)
                    s = s + node[0, rows, lanes] * arrived[rows, lanes]
                return s

            s = lax.fori_loop(0, tall // 8, inner, s)
        sums3[...] = row_of([s, (1.0 - up) * q, up * q])

    @pl.when(mid)
    def _():
        low, top = weights(0), weights(group)

        def strip(t, carry):
            rows = pl.ds(pl.multiple_of(t * 8, 8), 8)
            s, q, r = carry
            for c in range(width // 128):
                lanes = slice(c * 128, (c + 1) * 128)
                a = mix(low, range(group), rows, lanes)
                b = mix(top, range(group, 2 * group), rows, lanes)
                node[0, rows, lanes] = a
                node[1, rows, lanes] = b
                s, q, r = s + a * b, q + a * a, r + b * b
            return s, q, r

        s, q, r = lax.fori_loop(0, block // 8, strip, (zero,) * 3)
        sums3[...] = row_of([s, q, r])

    finish3, sent3 = gather(slots3, slot3_send, slot3_recv, slots3[dp * 2 + core])
    line = finish3()
    s = lane_value(line, 0)
    low = jnp.broadcast_to(1.0 - s / (2.0 * (lane_value(line, 1) + epsilon)), (8, width))
    top = jnp.broadcast_to(1.0 - s / (2.0 * (lane_value(line, 2) + epsilon)), (8, width))

    def last(first, second, other):
        def strip(t, carry):
            rows = pl.ds(pl.multiple_of(t * 8, 8), 8)
            comb[rows, :] = first * node[0, rows, :] + second * other[rows, :]
            return carry
        lax.fori_loop(0, block // 8, strip, 0)

    @pl.when(edge)
    def _():
        last((1.0 - up) * low + up * top, up * low + (1.0 - up) * top, arrived)

    @pl.when(mid)
    def _():
        last(low, top, node.at[1])

    mate_copy(dp, core).wait_send()
    for k in range(len(landed)):
        for i in landed[k][0]:
            mate_copy(spot(*i), core).wait_send()
        if k < len(common):
            for c in og_wave(k, common):
                c.wait_send()
    part.wait_send()

    @pl.when(mid)
    def _():
        for k in range(len(landed)):
            for i in landed[k][1]:
                mate_copy(spot(*i), core).wait_send()
            if k < len(common):
                for c in og_wave(k, extra):
                    c.wait_send()
                for kind, m in plan(k, 1):
                    act_copy(kind, m).wait_send()

    @pl.when(edge)
    def _():
        for k in range(len(common)):
            for kind, m in plan(k, 0):
                act_copy(kind, m).wait_send()
        for k in range(pieces):
            node_copy(k).wait_send()

    sent()
    sent3()


ORDER = (3, 1, 0, 2)
BATCHES = (
    (
        ((3, 4), (0, 3), (0, 2)),
        ((3, 5), (0, 1)),
        ((3, 6), (1, 3), (1, 2)),
        ((3, 7), (1, 1), (2, 4), (2, 5), (2, 6), (2, 7)),
    ),
    (
        ((3, 4), (0, 4), (2, 3), (2, 2)),
        ((3, 5), (0, 5), (2, 1)),
        ((3, 6), (0, 6)),
        ((3, 7), (0, 7), (1, 4), (1, 5), (1, 6), (1, 7)),
    ),
)


def exchange(n_dp, pre_act, out_weight, out_grad):
    tokens, hidden = pre_act.shape
    block = hidden // n_dp
    width = out_grad.shape[1]
    own_rows = out_grad.shape[0]
    step_cols = hidden // 8
    pieces = 4
    dma = pltpu.SemaphoreType.DMA
    hbm = pl.BlockSpec(memory_space=pl.ANY)
    vmem = pl.BlockSpec(memory_space=pltpu.VMEM)
    return pl.pallas_call(
        functools.partial(kernel, n_dp),
        out_shape=(
            jax.ShapeDtypeStruct((own_rows, width), jnp.bfloat16),
            jax.ShapeDtypeStruct((block, width), jnp.float32),
        ),
        in_specs=[hbm, hbm, hbm],
        out_specs=(vmem, vmem),
        scratch_shapes=[
            pltpu.VMEM((n_dp, tokens, block), jnp.bfloat16),
            pltpu.VMEM((n_dp, tokens, width), jnp.bfloat16),
            pltpu.VMEM((n_dp, block, width), jnp.float32),
            pltpu.VMEM((2, block, width), jnp.float32),
            pltpu.VMEM((block, width), jnp.float32),
            pltpu.VMEM((2, tokens, step_cols), jnp.bfloat16),
            pltpu.VMEM((2, step_cols, width), jnp.bfloat16),
            pltpu.VMEM((tokens, width), jnp.float32),
            pltpu.VMEM((own_rows, width), jnp.float32),
            pltpu.VMEM((128, 128), jnp.float32),
            pltpu.VMEM((2 * n_dp, 1, 128), jnp.float32),
            pltpu.VMEM((2 * n_dp, 1, 128), jnp.float32),
            pltpu.VMEM((n_dp, 128), jnp.float32),
            dma((16,)), dma((n_dp,)), dma((16,)), dma((n_dp,)), dma((n_dp,)), dma((n_dp,)), dma,
            dma((2, 2)), dma((2,)), dma((2 * n_dp,)), dma((2 * n_dp,)),
            dma((pieces,)), dma((pieces,)), dma((2 * n_dp,)), dma((2 * n_dp,)),
        ],
        compiler_params=pltpu.CompilerParams(
            collective_id=0, has_side_effects=True, vmem_limit_bytes=60 * 2**20
        ),
    )(pre_act, out_weight, out_grad)


def local(pre_act, out_weight, out_grad):
    n_dp = lax.axis_size("dp")
    block = pre_act.shape[1] // n_dp
    rows = out_grad.shape[0]
    if lax.axis_size("mp") == 2 and n_dp == 4 * len(ORDER) and block % 128 == 0 and rows % 16 == 0:
        return exchange(n_dp, pre_act, out_weight, out_grad)
    return halving(pre_act, out_weight, out_grad)


def solution(mesh):
    placed = (P("dp", "mp"), P("mp", None), P(("dp", "mp"), None))
    return jax.shard_map(
        local,
        mesh=mesh,
        in_specs=placed,
        out_specs=(P(("dp", "mp"), None), P(("mp", "dp"), None)),
        check_vma=False,
    )
```

time: 197 us -> 206 us (1.046)
  Pallas kernels: 192 us -> 201 us
    pallas_call x1, Pallas kernels: 192 us -> 201 us  [exchange(): pl.pallas_call(functools.partial(kernel, n_dp), out_shape=(jax.ShapeDtype...]
where the time goes in v1:
time: 206 us
  Pallas kernels  201 us (98%)
  local copies, waits for them, and re-layouts  3.93 us (2%)
    pallas_call x1, Pallas kernels, exchange(): pl.pallas_call(functools.partial(kernel, n_dp), out_shape=(jax.ShapeDtype...  201 us

profile of v1, /device:TPU:0, one launch (start us, length us, event | category | flops | bytes accessed | tf_op | source)
XLA Modules:
  0.0 205.7 jit_solution(12095223771739161894)
XLA Ops:
  0.6 201.2 %shard_map.50 = (bf16[256,512]{1,0:T(8,128)(2,1)}, f32[512,512]{1,0:T(8,128)}) custom-call(bf16[512,8192]{1,0:T(8,128)(2,1)} %pre.1, bf16[8192,512]{1,0:T(8,128)(2,1)} %w.1, bf16[256,512]{1,0:T(8,128)(2,1)} %og.1), custom_call_target="tpu_custom_call" | custom-call | tf_op jit(solution)/shard_map/pallas_call | solution.py:605
  201.8 1.7 copy.7
  203.5 2.3 %copy.8 = f32[512,512]{1,0:T(8,128)} copy(f32[512,512]{1,0:T(8,128)} %get-tuple-element.5) | data formatting | bytes 2097152

commit v2 on v1

--- a/solution.py
+++ b/solution.py
@@ -248,25 +248,24 @@
     og_local.wait()
     pl.semaphore_wait(barrier, 2 * n_dp - 1)
 
-    cross, along = 2 - core, 1 + core
     common = (
-        ((z, 0, z, 1), (z, 0, z, 2), (z, 0, zi, 0)),
-        ((z, cross, z, along), (z, 1, zi, 0), (z, 2, zi, 0)),
-        ((z, 3, zi, 0),),
-        (),
+        ((z, 0, far_mid_z, 0), (z, 0, zi, 0), (z, 0, z, 3), (z, 0, z, 1), (z, 0, z, 2)),
+        ((z, 1, zi, 0), (z, 2, zi, 0), (z, 3, zi, 0)),
     )
     extra = (
-        ((z, 0, far_mid_z, 0),),
-        ((zi, 0, far_mid_z, 0), (far_mid_z, 0, z, 1), (far_mid_z, 0, z, 2)),
-        ((z, 3, far_mid_z, 0), (far_edge_z, 0, z, 1), (far_edge_z, 0, z, 2)),
-        ((far_edge_z, cross, z, along),),
+        (),
+        (
+            (z, 1, far_mid_z, 0), (z, 2, far_mid_z, 0), (z, 3, far_mid_z, 0),
+            (far_edge_z, 0, z, 3), (far_edge_z, 0, z, 1), (far_edge_z, 0, z, 2),
+        ),
     )
     landed = (
         ((), ()),
-        (((z, 1), (z, 2), (zi, 0)), ((far_mid_z, 0),)),
-        (((z, 3), (zi, 1), (zi, 2)), ((far_edge_z, 0), (far_mid_z, 1), (far_mid_z, 2))),
-        (((zi, 3),), ((far_mid_z, 3), (far_edge_z, 1), (far_edge_z, 2))),
-        ((), ((far_edge_z, 3),)),
+        (((z, 1), (z, 2), (z, 3), (zi, 0)), ((far_mid_z, 0), (far_edge_z, 0))),
+        (
+            ((zi, 1), (zi, 2), (zi, 3)),
+            tuple((far_mid_z, m) for m in (1, 2, 3)) + tuple((far_edge_z, m) for m in (1, 2, 3)),
+        ),
     )
 
     def og_wave(k, moves):
@@ -331,8 +330,6 @@
     part.wait_recv()
     proj[...] = (acc[pl.ds(core * own_rows, own_rows), :] + part_in[...]).astype(proj.dtype)
     wave(2)
-    wave(3)
-    wave(4)
 
     def settle(i):
         mate_copy(i, mate).wait_recv()
@@ -578,16 +575,18 @@
 ORDER = (3, 1, 0, 2)
 BATCHES = (
     (
-        ((3, 4), (0, 3), (0, 2)),
-        ((3, 5), (0, 1)),
-        ((3, 6), (1, 3), (1, 2)),
-        ((3, 7), (1, 1), (2, 4), (2, 5), (2, 6), (2, 7)),
+        ((3, 4),),
+        (
+            (3, 5), (3, 6), (3, 7), (2, 4), (2, 5), (2, 6), (2, 7),
+            (0, 3), (0, 2), (0, 1), (1, 3), (1, 2), (1, 1),
+        ),
     ),
     (
-        ((3, 4), (0, 4), (2, 3), (2, 2)),
-        ((3, 5), (0, 5), (2, 1)),
-        ((3, 6), (0, 6)),
-        ((3, 7), (0, 7), (1, 4), (1, 5), (1, 6), (1, 7)),
+        ((3, 4), (0, 4)),
+        (
+            (3, 5), (0, 5), (3, 6), (0, 6), (3, 7), (0, 7), (1, 4), (1, 5), (1, 6), (1, 7),
+            (2, 3), (2, 2), (2, 1),
+        ),
     ),
 )
 

time: 206 us -> 175 us (0.85)
  Pallas kernels: 201 us -> 170 us
    pallas_call x1, Pallas kernels: 201 us -> 170 us  [exchange(): pl.pallas_call(functools.partial(kernel, n_dp), out_shape=(jax.ShapeDtype...]
where the time goes in v2:
time: 175 us
  Pallas kernels  170 us (97%)
  local copies, waits for them, and re-layouts  3.93 us (2%)
    pallas_call x1, Pallas kernels, exchange(): pl.pallas_call(functools.partial(kernel, n_dp), out_shape=(jax.ShapeDtype...  170 us
    unnamed x2, local copies, waits for them, and re-layouts  3.93 us

profile of v2, /device:TPU:0, one launch (start us, length us, event | category | flops | bytes accessed | tf_op | source)
XLA Modules:
  0.0 174.7 jit_solution(17068401849815061161)
XLA Ops:
  0.6 170.2 %shard_map.50 = (bf16[256,512]{1,0:T(8,128)(2,1)}, f32[512,512]{1,0:T(8,128)}) custom-call(bf16[512,8192]{1,0:T(8,128)(2,1)} %pre.1, bf16[8192,512]{1,0:T(8,128)(2,1)} %w.1, bf16[256,512]{1,0:T(8,128)(2,1)} %og.1), custom_call_target="tpu_custom_call" | custom-call | tf_op jit(solution)/shard_map/pallas_call | solution.py:604
  170.8 1.7 copy.7
  172.5 2.3 %copy.8 = f32[512,512]{1,0:T(8,128)} copy(f32[512,512]{1,0:T(8,128)} %get-tuple-element.5) | data formatting | bytes 2097152

commit v3 on v2

--- a/solution.py
+++ b/solution.py
@@ -142,7 +142,7 @@
     n_dp, pre, w, og, proj, comb,
     acts, grads, leaf, node, arrived, xbuf, wbuf, acc, part_in, gsum, slots, slots3, coefs,
     act_send, act_recv, og_send, og_recv, mate_send, mate_recv, local_sem,
-    fwd_sem, part_sem, slot_send, slot_recv, node_send, node_recv, slot3_send, slot3_recv,
+    fwd_sem, part_sem, slot_send, slot_recv, node_send, node_recv, slot3_send, slot3_recv, ready,
 ):
     dp = lax.axis_index("dp")
     core = lax.axis_index("mp")
@@ -173,15 +173,23 @@
         return k
 
     barrier = pltpu.get_barrier_semaphore()
-    for q in range(1, 2 * n_dp):
-        other = lax.rem(dp * 2 + core + q, 2 * n_dp)
-        pl.semaphore_signal(
-            barrier, inc=1, device_id=(other // 2, lax.rem(other, 2)), device_id_type=MESH
-        )
+
+    def greet(sem, to, side):
+        pl.semaphore_signal(sem, inc=1, device_id=(to, side), device_id_type=MESH)
+
+    beside, behind, above, across = spot(z, 1), spot(z, 2), spot(zi, 0), spot(far_mid_z, 0)
+    for to in (beside, behind, above):
+        greet(barrier, to, core)
+    greet(barrier, dp, mate)
+
+    @pl.when(mid)
+    def _():
+        greet(barrier, across, core)
 
     def half(i, side):
         return grads.at[i, pl.ds(side * own_rows, own_rows)]
 
+    home = dp
     og_local = pltpu.make_async_copy(og, half(dp, core), local_sem)
     og_local.start()
 
@@ -208,7 +216,7 @@
 
     def og_copy(n, i, to):
         return pltpu.make_async_remote_copy(
-            src_ref=half(i, core), dst_ref=half(i, core), send_sem=og_send.at[n],
+            src_ref=og if i is home else half(i, core), dst_ref=half(i, core), send_sem=og_send.at[n],
             recv_sem=og_recv.at[i], device_id=(to, core), device_id_type=MESH,
         )
 
@@ -245,11 +253,12 @@
                 for kind, m in plan(batch, where):
                     act_copy(kind, m).start()
 
-    og_local.wait()
-    pl.semaphore_wait(barrier, 2 * n_dp - 1)
+    def meet(n, to, side):
+        greet(ready.at[n], to, side)
+        pl.semaphore_wait(ready.at[n], 1)
 
     common = (
-        ((z, 0, far_mid_z, 0), (z, 0, zi, 0), (z, 0, z, 3), (z, 0, z, 1), (z, 0, z, 2)),
+        ((z, 0, zi, 0), (z, 0, z, 1), (z, 0, z, 2), (z, 0, far_mid_z, 0), (z, 0, z, 3)),
         ((z, 1, zi, 0), (z, 2, zi, 0), (z, 3, zi, 0)),
     )
     extra = (
@@ -271,7 +280,7 @@
     def og_wave(k, moves):
         base = sum(len(c) for c in moves[:k])
         base += sum(len(c) for c in common) if moves is extra else 0
-        return [og_copy(base + n, spot(a, m), spot(b, r)) for n, (a, m, b, r) in enumerate(moves[k])]
+        return [og_copy(base + n, home if a is z and m == 0 else spot(a, m), spot(b, r)) for n, (a, m, b, r) in enumerate(moves[k])]
 
     def wave(k):
         for i in landed[k][0]:
@@ -293,8 +302,37 @@
 
             send_acts(k)
 
-    wave(0)
+    first = og_wave(0, common)
+
+    @pl.when(edge)
+    def _():
+        pl.semaphore_wait(barrier, 4)
+
+    @pl.when(mid)
+    def _():
+        pl.semaphore_wait(barrier, 5)
+        first[3].start()
+
+    for c in first[:3]:
+        c.start()
+    og_local.wait()
     mate_copy(dp, core).start()
+    meet(0, beside, core)
+    meet(1, behind, core)
+    first[4].start()
+    meet(2, dp, mate)
+
+    @pl.when(mid)
+    def _():
+        meet(3, across, core)
+
+    meet(4, above, core)
+
+    @pl.when(edge)
+    def _():
+        first[3].start()
+
+    send_acts(0)
 
     @pl.when(edge)
     def _():
@@ -394,7 +432,6 @@
             gram((i, i), seen)
             seen.append((i, i))
 
-        home = spot(z, 0)
         take(home, near)
         for m in (3, 2, 1):
             take(spot(z, m), near)
@@ -418,27 +455,40 @@
             copy(q, lax.rem(mine + q, 2 * n_dp), mine).start()
             return carry
 
-        def take(q, carry):
-            other = lax.rem(mine + q, 2 * n_dp)
-            copy(q, other, other).wait_recv()
-            return carry
-
         def left(q, carry):
             copy(q, lax.rem(mine + q, 2 * n_dp), mine).wait_send()
             return carry
 
-        def finish():
-            lax.fori_loop(1, 2 * n_dp, take, 0)
-            total = buf[0]
-            for k in range(1, 2 * n_dp):
-                total = total + buf[k]
+        def settled(first, count):
+            def take(k, carry):
+                @pl.when(first + k != mine)
+                def _():
+                    copy(0, first + k, first + k).wait_recv()
+                return carry
+
+            lax.fori_loop(0, count, take, 0)
+
+        def finish(first, count):
+            settled(first, count)
+            total = buf[first]
+            for k in range(1, count):
+                total = total + buf[first + k]
             return total
 
-        lax.fori_loop(1, 2 * n_dp, go, 0)
-        return finish, lambda: lax.fori_loop(1, 2 * n_dp, left, 0)
-
-    finish, sent = gather(slots, slot_send, slot_recv, line_of(gsum[...]))
-    coefs[...] = tree_coefs(finish(), group)
+        lax.fori_loop(n_dp, 2 * n_dp, go, 0)
+        lax.fori_loop(1, n_dp, go, 0)
+        return finish, settled, lambda: lax.fori_loop(1, 2 * n_dp, left, 0)
+
+    finish, settled, sent = gather(slots, slot_send, slot_recv, line_of(gsum[...]))
+    plane = n_dp // 2
+
+    @pl.when(edge)
+    def _():
+        coefs[...] = tree_coefs(finish(high * plane, 3 * plane), group)
+
+    @pl.when(mid)
+    def _():
+        coefs[...] = tree_coefs(finish(0, 2 * n_dp), group)
 
     def weights(first):
         return [jnp.broadcast_to(coefs[pl.ds(first + k, 1), :], (8, 128)) for k in range(group)]
@@ -519,8 +569,8 @@
         s, q, r = lax.fori_loop(0, block // 8, strip, (zero,) * 3)
         sums3[...] = row_of([s, q, r])
 
-    finish3, sent3 = gather(slots3, slot3_send, slot3_recv, slots3[dp * 2 + core])
-    line = finish3()
+    finish3, _, sent3 = gather(slots3, slot3_send, slot3_recv, slots3[dp * 2 + core])
+    line = finish3(0, 2 * n_dp)
     s = lane_value(line, 0)
     low = jnp.broadcast_to(1.0 - s / (2.0 * (lane_value(line, 1) + epsilon)), (8, width))
     top = jnp.broadcast_to(1.0 - s / (2.0 * (lane_value(line, 2) + epsilon)), (8, width))
@@ -539,6 +589,10 @@
     @pl.when(mid)
     def _():
         last(low, top, node.at[1])
+
+    @pl.when(edge)
+    def _():
+        settled(far_edge_z * plane, plane)
 
     mate_copy(dp, core).wait_send()
     for k in range(len(landed)):
@@ -626,9 +680,10 @@
             dma((16,)), dma((n_dp,)), dma((16,)), dma((n_dp,)), dma((n_dp,)), dma((n_dp,)), dma,
             dma((2, 2)), dma((2,)), dma((2 * n_dp,)), dma((2 * n_dp,)),
             dma((pieces,)), dma((pieces,)), dma((2 * n_dp,)), dma((2 * n_dp,)),
+            pltpu.SemaphoreType.REGULAR((5,)),
         ],
         compiler_params=pltpu.CompilerParams(
-            collective_id=0, has_side_effects=True, vmem_limit_bytes=60 * 2**20
+            collective_id=0, has_side_effects=True, vmem_limit_bytes=52 * 2**20
         ),
     )(pre_act, out_weight, out_grad)
 

time: 175 us -> 171 us (0.977)
  Pallas kernels: 170 us -> 168 us
    pallas_call x1, Pallas kernels: 170 us -> 168 us  [exchange(): pl.pallas_call(functools.partial(kernel, n_dp), out_shape=(jax.ShapeDtype...]
    unnamed x2 -> x4, local copies, waits for them, and re-layouts: 3.93 us -> 2.62 us
where the time goes in v3:
time: 171 us
  Pallas kernels  168 us (98%)
  local copies, waits for them, and re-layouts  2.62 us (2%)
    pallas_call x1, Pallas kernels, exchange(): pl.pallas_call(functools.partial(kernel, n_dp), out_shape=(jax.ShapeDtype...  168 us

profile of v3, /device:TPU:0, one launch (start us, length us, event | category | flops | bytes accessed | tf_op | source)
XLA Modules:
  0.0 171.0 jit_solution(9823770036960669717)
XLA Ops:
  0.6 0.0 copy-start
  0.6 0.9 copy-done
  1.6 167.8 %shard_map.50 = (bf16[256,512]{1,0:T(8,128)(2,1)S(1)}, f32[512,512]{1,0:T(8,128)S(1)}) custom-call(bf16[512,8192]{1,0:T(8,128)(2,1)} %pre.1, bf16[8192,512]{1,0:T(8,128)(2,1)} %w.1, bf16[256,512]{1,0:T(8,128)(2,1)S(1)} %copy-done), custom_call_target="tpu_custom_call" | custom-call | tf_op jit(solution)/shard_map/pallas_call | solution.py:658
  169.4 0.7 copy.7
  170.1 1.0 copy.8
Async XLA Ops:
  0.6 1.0 copy-start

commit v4 on v3

--- a/solution.py
+++ b/solution.py
@@ -216,13 +216,13 @@
 
     def og_copy(n, i, to):
         return pltpu.make_async_remote_copy(
-            src_ref=og if i is home else half(i, core), dst_ref=half(i, core), send_sem=og_send.at[n],
+            src_ref=og if i is home else half(i, core), dst_ref=half(i, core), send_sem=og_send,
             recv_sem=og_recv.at[i], device_id=(to, core), device_id_type=MESH,
         )
 
     def mate_copy(i, side):
         return pltpu.make_async_remote_copy(
-            src_ref=half(i, side), dst_ref=half(i, side), send_sem=mate_send.at[i],
+            src_ref=half(i, side), dst_ref=half(i, side), send_sem=mate_send,
             recv_sem=mate_recv.at[i], device_id=(dp, mate), device_id_type=MESH,
         )
 
@@ -239,7 +239,7 @@
             b, slot = to, dp
         return pltpu.make_async_remote_copy(
             src_ref=pre.at[:, cols(b)], dst_ref=acts.at[slot],
-            send_sem=act_send.at[kind * 4 + m], recv_sem=act_recv.at[slot],
+            send_sem=act_send, recv_sem=act_recv.at[slot],
             device_id=(to, core), device_id_type=MESH,
         )
 
@@ -317,21 +317,15 @@
         c.start()
     og_local.wait()
     mate_copy(dp, core).start()
-    meet(0, beside, core)
-    meet(1, behind, core)
+    meet(0, above, core)
+
+    @pl.when(edge)
+    def _():
+        first[3].start()
+
+    meet(1, beside, core)
+    meet(2, behind, core)
     first[4].start()
-    meet(2, dp, mate)
-
-    @pl.when(mid)
-    def _():
-        meet(3, across, core)
-
-    meet(4, above, core)
-
-    @pl.when(edge)
-    def _():
-        first[3].start()
-
     send_acts(0)
 
     @pl.when(edge)
@@ -365,6 +359,13 @@
     )
     part.start()
     wave(1)
+    meet(3, dp, mate)
+
+    @pl.when(mid)
+    def _():
+        meet(4, across, core)
+
+    meet(5, above, core)
     part.wait_recv()
     proj[...] = (acc[pl.ds(core * own_rows, own_rows), :] + part_in[...]).astype(proj.dtype)
     wave(2)
@@ -377,7 +378,7 @@
             self_copy(0, slot).wait()
         else:
             pltpu.make_async_remote_copy(
-                src_ref=pre.at[:, cols(0)], dst_ref=acts.at[slot], send_sem=act_send.at[0],
+                src_ref=pre.at[:, cols(0)], dst_ref=acts.at[slot], send_sem=act_send,
                 recv_sem=act_recv.at[slot], device_id=(dp, mate), device_id_type=MESH,
             ).wait_recv()
         a = jnp.maximum(acts[slot], jnp.zeros((), jnp.bfloat16))
@@ -441,59 +442,66 @@
             take(spot(far_mid_z, turn(j)), away)
             take(spot(zi, turn(j)), near)
 
+    plane = n_dp // 2
+
     def gather(buf, send, recv, line):
         mine = dp * 2 + core
         buf[mine] = line
 
-        def copy(q, other, at):
+        def copy(other, at):
             return pltpu.make_async_remote_copy(
-                src_ref=buf.at[at], dst_ref=buf.at[at], send_sem=send.at[q], recv_sem=recv.at[at],
+                src_ref=buf.at[at], dst_ref=buf.at[at], send_sem=send, recv_sem=recv.at[at // plane],
                 device_id=(other // 2, lax.rem(other, 2)), device_id_type=MESH,
             )
 
         def go(q, carry):
-            copy(q, lax.rem(mine + q, 2 * n_dp), mine).start()
+            copy(lax.rem(mine + q, 2 * n_dp), mine).start()
             return carry
 
-        def left(q, carry):
-            copy(q, lax.rem(mine + q, 2 * n_dp), mine).wait_send()
-            return carry
+        def landing(at_z, rows):
+            here = buf.at[pl.ds(0, rows)]
+            return pltpu.make_async_remote_copy(
+                src_ref=here, dst_ref=here, send_sem=send, recv_sem=recv.at[at_z],
+                device_id=(dp, mate), device_id_type=MESH,
+            )
 
         def settled(first, count):
-            def take(k, carry):
-                @pl.when(first + k != mine)
+            for k in range(count):
+                at_z = first + k
+
+                @pl.when(at_z == z)
                 def _():
-                    copy(0, first + k, first + k).wait_recv()
-                return carry
-
-            lax.fori_loop(0, count, take, 0)
+                    landing(at_z, plane - 1).wait_recv()
+
+                @pl.when(at_z != z)
+                def _():
+                    landing(at_z, plane).wait_recv()
 
         def finish(first, count):
             settled(first, count)
-            total = buf[first]
-            for k in range(1, count):
-                total = total + buf[first + k]
+            total = buf[first * plane]
+            for k in range(1, count * plane):
+                total = total + buf[first * plane + k]
             return total
 
         lax.fori_loop(n_dp, 2 * n_dp, go, 0)
         lax.fori_loop(1, n_dp, go, 0)
-        return finish, settled, lambda: lax.fori_loop(1, 2 * n_dp, left, 0)
+        return finish, settled, landing(0, 2 * n_dp - 1).wait_send
 
     finish, settled, sent = gather(slots, slot_send, slot_recv, line_of(gsum[...]))
-    plane = n_dp // 2
-
-    @pl.when(edge)
-    def _():
-        coefs[...] = tree_coefs(finish(high * plane, 3 * plane), group)
-
-    @pl.when(mid)
-    def _():
-        coefs[...] = tree_coefs(finish(0, 2 * n_dp), group)
+
+    @pl.when(edge)
+    def _():
+        coefs[...] = tree_coefs(finish(high, 3), group)
+
+    @pl.when(mid)
+    def _():
+        coefs[...] = tree_coefs(finish(0, 4), group)
 
     def weights(first):
         return [jnp.broadcast_to(coefs[pl.ds(first + k, 1), :], (8, 128)) for k in range(group)]
 
-    pieces = node_send.shape[0]
+    pieces = node_recv.shape[0]
     tall = block // pieces
 
     def mix(weight, places, rows, lanes):
@@ -509,7 +517,7 @@
         rows = pl.ds(k * tall, tall)
         return pltpu.make_async_remote_copy(
             src_ref=node.at[1, rows], dst_ref=arrived.at[rows],
-            send_sem=node_send.at[k], recv_sem=node_recv.at[k],
+            send_sem=node_send, recv_sem=node_recv.at[k],
             device_id=(far, core), device_id_type=MESH,
         )
 
@@ -570,7 +578,7 @@
         sums3[...] = row_of([s, q, r])
 
     finish3, _, sent3 = gather(slots3, slot3_send, slot3_recv, slots3[dp * 2 + core])
-    line = finish3(0, 2 * n_dp)
+    line = finish3(0, 4)
     s = lane_value(line, 0)
     low = jnp.broadcast_to(1.0 - s / (2.0 * (lane_value(line, 1) + epsilon)), (8, width))
     top = jnp.broadcast_to(1.0 - s / (2.0 * (lane_value(line, 2) + epsilon)), (8, width))
@@ -592,35 +600,33 @@
 
     @pl.when(edge)
     def _():
-        settled(far_edge_z * plane, plane)
-
-    mate_copy(dp, core).wait_send()
-    for k in range(len(landed)):
-        for i in landed[k][0]:
-            mate_copy(spot(*i), core).wait_send()
-        if k < len(common):
-            for c in og_wave(k, common):
-                c.wait_send()
+        settled(far_edge_z, 1)
+
+    def drained(send, ref, count):
+        rows = ref.at[pl.ds(0, count)]
+        pltpu.make_async_remote_copy(
+            src_ref=rows, dst_ref=rows, send_sem=send, recv_sem=part_sem.at[1],
+            device_id=(dp, mate), device_id_type=MESH,
+        ).wait_send()
+
     part.wait_send()
 
     @pl.when(mid)
     def _():
-        for k in range(len(landed)):
-            for i in landed[k][1]:
-                mate_copy(spot(*i), core).wait_send()
-            if k < len(common):
-                for c in og_wave(k, extra):
-                    c.wait_send()
-                for kind, m in plan(k, 1):
-                    act_copy(kind, m).wait_send()
-
-    @pl.when(edge)
-    def _():
-        for k in range(len(common)):
-            for kind, m in plan(k, 0):
-                act_copy(kind, m).wait_send()
-        for k in range(pieces):
-            node_copy(k).wait_send()
+        drained(og_send, grads, 7)
+        drained(mate_send, grads, group)
+        drained(act_send, acts, n_dp - 1)
+
+    @pl.when(edge)
+    def _():
+        drained(og_send, grads, 4)
+        drained(mate_send, grads, group // 2)
+        drained(act_send, acts, n_dp - 2)
+        node_sent = pltpu.make_async_remote_copy(
+            src_ref=node.at[1], dst_ref=arrived, send_sem=node_send, recv_sem=node_recv.at[0],
+            device_id=(far, core), device_id_type=MESH,
+        )
+        node_sent.wait_send()
 
     sent()
     sent3()
@@ -677,10 +683,9 @@
             pltpu.VMEM((2 * n_dp, 1, 128), jnp.float32),
             pltpu.VMEM((2 * n_dp, 1, 128), jnp.float32),
             pltpu.VMEM((n_dp, 128), jnp.float32),
-            dma((16,)), dma((n_dp,)), dma((16,)), dma((n_dp,)), dma((n_dp,)), dma((n_dp,)), dma,
-            dma((2, 2)), dma((2,)), dma((2 * n_dp,)), dma((2 * n_dp,)),
-            dma((pieces,)), dma((pieces,)), dma((2 * n_dp,)), dma((2 * n_dp,)),
-            pltpu.SemaphoreType.REGULAR((5,)),
+            dma, dma((n_dp,)), dma, dma((n_dp,)), dma, dma((n_dp,)), dma,
+            dma((2, 2)), dma((2,)), dma, dma((4,)), dma, dma((pieces,)), dma, dma((4,)),
+            pltpu.SemaphoreType.REGULAR((6,)),
         ],
         compiler_params=pltpu.CompilerParams(
             collective_id=0, has_side_effects=True, vmem_limit_bytes=52 * 2**20

time: 171 us -> 170 us (level)
  Pallas kernels: 168 us -> 166 us
    pallas_call x1, Pallas kernels: 168 us -> 166 us  [exchange(): pl.pallas_call(functools.partial(kernel, n_dp), out_shape=(jax.ShapeDtype...]
where the time goes in v4:
time: 170 us; the launch traced here: 169 us
  Pallas kernels  166 us (98%)
  local copies, waits for them, and re-layouts  2.62 us (2%)
    pallas_call x1, Pallas kernels, exchange(): pl.pallas_call(functools.partial(kernel, n_dp), out_shape=(jax.ShapeDtype...  166 us

profile of v4, /device:TPU:0, one launch (start us, length us, event | category | flops | bytes accessed | tf_op | source)
XLA Modules:
  0.0 169.3 jit_solution(6982240009440104856)
XLA Ops:
  0.6 0.0 copy-start
  0.6 0.9 copy-done
  1.6 166.0 %shard_map.50 = (bf16[256,512]{1,0:T(8,128)(2,1)S(1)}, f32[512,512]{1,0:T(8,128)S(1)}) custom-call(bf16[512,8192]{1,0:T(8,128)(2,1)} %pre.1, bf16[8192,512]{1,0:T(8,128)(2,1)} %w.1, bf16[256,512]{1,0:T(8,128)(2,1)S(1)} %copy-done), custom_call_target="tpu_custom_call" | custom-call | tf_op jit(solution)/shard_map/pallas_call | solution.py:664
  167.6 0.7 copy.7
  168.3 1.0 copy.8
Async XLA Ops:
  0.6 1.0 copy-start

commit v5 on v4

--- a/solution.py
+++ b/solution.py
@@ -389,15 +389,15 @@
         seen = others + [new]
 
         def strip(t, carry):
-            rows = pl.ds(pl.multiple_of(t * 8, 8), 8)
-            for c in range(width // 128):
-                lanes = slice(c * 128, (c + 1) * 128)
+            for n in range(width // 128 * 4):
+                rows = pl.ds(pl.multiple_of(t * 32 + n % 4 * 8, 8), 8)
+                lanes = slice(n // 4 * 128, (n // 4 + 1) * 128)
                 v = leaf[slot, rows, lanes]
                 carry = tuple(s + v * leaf[o, rows, lanes] for s, (_, o) in zip(carry, seen[:-1])) + (carry[-1] + v * v,)
             return carry
 
         zero = jnp.zeros((8, 128), jnp.float32)
-        sums = lax.fori_loop(0, block // 8, strip, (zero,) * len(seen))
+        sums = lax.fori_loop(0, block // 32, strip, (zero,) * len(seen))
         for s, (j, _) in zip(sums, seen):
             line = jnp.sum(s, axis=0, keepdims=True)
             for p, q in ((i, j), (j, i))[: 1 if j is i else 2]:
@@ -637,7 +637,7 @@
     (
         ((3, 4),),
         (
-            (3, 5), (3, 6), (3, 7), (2, 4), (2, 5), (2, 6), (2, 7),
+            (2, 4), (3, 5), (2, 5), (3, 6), (2, 6), (3, 7), (2, 7),
             (0, 3), (0, 2), (0, 1), (1, 3), (1, 2), (1, 1),
         ),
     ),
@@ -667,7 +667,7 @@
             jax.ShapeDtypeStruct((own_rows, width), jnp.bfloat16),
             jax.ShapeDtypeStruct((block, width), jnp.float32),
         ),
-        in_specs=[hbm, hbm, hbm],
+        in_specs=[hbm, hbm, pl.BlockSpec(memory_space=pltpu.HBM)],
         out_specs=(vmem, vmem),
         scratch_shapes=[
             pltpu.VMEM((n_dp, tokens, block), jnp.bfloat16),

time: 170 us -> 168 us (0.988)
  Pallas kernels: 166 us -> 164 us
where the time goes in v5:
time: 168 us
  Pallas kernels  164 us (98%)
  local copies, waits for them, and re-layouts  2.62 us (2%)
    pallas_call x1, Pallas kernels, exchange(): pl.pallas_call(functools.partial(kernel, n_dp), out_shape=(jax.ShapeDtype...  164 us

profile of v5, /device:TPU:0, one launch (start us, length us, event | category | flops | bytes accessed | tf_op | source)
XLA Modules:
  0.0 167.7 jit_solution(2426806671828895347)
XLA Ops:
  0.6 0.0 copy-start
  0.6 0.9 copy-done
  1.6 164.4 %shard_map.50 = (bf16[256,512]{1,0:T(8,128)(2,1)S(1)}, f32[512,512]{1,0:T(8,128)S(1)}) custom-call(bf16[512,8192]{1,0:T(8,128)(2,1)} %pre.1, bf16[8192,512]{1,0:T(8,128)(2,1)} %w.1, bf16[256,512]{1,0:T(8,128)(2,1)S(1)} %copy-done), custom_call_target="tpu_custom_call" | custom-call | tf_op jit(solution)/shard_map/pallas_call | solution.py:664
  166.0 0.7 copy.7
  166.7 1.0 copy.8
Async XLA Ops:
  0.6 1.0 copy-start

commit v6 on v5

--- a/solution.py
+++ b/solution.py
@@ -112,12 +112,16 @@
     return jnp.where((at // bit) % 2 == 0, up, down)
 
 
-def tree_coefs(line, group):
-    rows = 2 * group
+def tree_coefs(line, group, side):
     lanes = line.shape[1]
-    m = jnp.concatenate([pltpu.roll(jnp.broadcast_to(line, (8, lanes)), group * r, 1)[0:1] if r else line for r in range(rows)], axis=0)
+    m = jnp.broadcast_to(line, (group, lanes))
+    turned = pltpu.roll(m, group * group, 1)
+    m = (turned if side else m) if isinstance(side, int) else jnp.where(side == 1, turned, m)
     lane = lax.broadcasted_iota(jnp.int32, m.shape, 1)
-    own = lax.broadcasted_iota(jnp.int32, m.shape, 0) % group
+    own = lax.broadcasted_iota(jnp.int32, m.shape, 0)
+    for level in range(group.bit_length() - 1):
+        bit = 2**level
+        m = jnp.where((own // bit) % 2 == 1, pltpu.roll(m, group * bit, 1), m)
     coef = jnp.ones_like(m)
     for level in range(group.bit_length() - 1):
         bit = 2**level
@@ -127,14 +131,11 @@
         f = 1.0 - inner / (2.0 * (jnp.maximum(square, 0.0) + epsilon))
         f = jnp.broadcast_to(f, m.shape)
         coef = coef * f
-        across = jnp.where(lane == own, f, 0.0)
-        across = jnp.concatenate(
-            [jnp.broadcast_to(jnp.sum(across[g * group:(g + 1) * group], axis=0, keepdims=True), (group, lanes)) for g in range(2)],
-            axis=0,
-        )
-        m = m * f * across
-        m = m + swap(m, 1, bit)
-        m = m + swap(m, 0, bit)
+        if 2 * bit < group:
+            across = jnp.sum(jnp.where(lane == own, f, 0.0), axis=0, keepdims=True)
+            m = m * f * jnp.broadcast_to(across, m.shape)
+            m = m + swap(m, 1, bit)
+            m = m + swap(m, 0, bit)
     return coef
 
 
@@ -368,7 +369,6 @@
     meet(5, above, core)
     part.wait_recv()
     proj[...] = (acc[pl.ds(core * own_rows, own_rows), :] + part_in[...]).astype(proj.dtype)
-    wave(2)
 
     def settle(i):
         mate_copy(i, mate).wait_recv()
@@ -413,6 +413,8 @@
 
                 @pl.when(h == 0)
                 def _():
+                    for late in landed[2][0] if n == 4 else ():
+                        og_arrival(spot(*late))
                     settle(i)
 
                 slot = lax.rem(i, group) * 2 + h
@@ -436,6 +438,8 @@
         take(home, near)
         for m in (3, 2, 1):
             take(spot(z, m), near)
+        for late in landed[2][0] + landed[2][1]:
+            og_arrival(spot(*late))
         for j in range(4):
             take(spot(far_edge_z, turn(j)), away)
         for j in range(4):
@@ -492,11 +496,13 @@
 
     @pl.when(edge)
     def _():
-        coefs[...] = tree_coefs(finish(high, 3), group)
-
-    @pl.when(mid)
-    def _():
-        coefs[...] = tree_coefs(finish(0, 4), group)
+        coefs[pl.ds(pl.multiple_of(high * group, group), group), :] = tree_coefs(finish(high, 3), group, high)
+
+    @pl.when(mid)
+    def _():
+        total = finish(0, 4)
+        for side in range(2):
+            coefs[side * group:(side + 1) * group, :] = tree_coefs(total, group, side)
 
     def weights(first):
         return [jnp.broadcast_to(coefs[pl.ds(first + k, 1), :], (8, 128)) for k in range(group)]
@@ -690,7 +696,7 @@
         compiler_params=pltpu.CompilerParams(
             collective_id=0, has_side_effects=True, vmem_limit_bytes=52 * 2**20
         ),
-    )(pre_act, out_weight, out_grad)
+    )(pre_act, out_weight, pltpu.with_memory_space_constraint(out_grad, pltpu.HBM))
 
 
 def local(pre_act, out_weight, out_grad):

time: 168 us -> 167 us (level)
  no operation moved by 1% of the time
where the time goes in v6:
time: 167 us
  Pallas kernels  165 us (99%)
  local copies, waits for them, and re-layouts  1.67 us (1%)
    pallas_call x1, Pallas kernels, exchange(): pl.pallas_call(functools.partial(kernel, n_dp), out_shape=(jax.ShapeDtype...  165 us

profile of v6, /device:TPU:0, one launch (start us, length us, event | category | flops | bytes accessed | tf_op | source)
XLA Modules:
  0.0 167.2 jit_solution(1359334537333050514)
XLA Ops:
  0.6 164.9 %shard_map.50 = (bf16[256,512]{1,0:T(8,128)(2,1)S(1)}, f32[512,512]{1,0:T(8,128)S(1)}) custom-call(bf16[512,8192]{1,0:T(8,128)(2,1)} %pre.1, bf16[8192,512]{1,0:T(8,128)(2,1)} %w.1, bf16[256,512]{1,0:T(8,128)(2,1)} %og.1), custom_call_target="tpu_custom_call" | custom-call | tf_op jit(solution)/shard_map/pallas_call | solution.py:670
  165.5 0.7 copy.7
  166.2 1.0 copy.8

commit v7 on v6

--- a/solution.py
+++ b/solution.py
@@ -352,14 +352,15 @@
         acc[...] += jnp.dot(v, wbuf[slot], preferred_element_type=jnp.float32)
         return carry
 
-    lax.fori_loop(0, steps, forward, 0)
+    lax.fori_loop(0, steps // 2, forward, 0)
+    wave(1)
+    lax.fori_loop(steps // 2, steps, forward, 0)
     part = pltpu.make_async_remote_copy(
         src_ref=acc.at[pl.ds(mate * own_rows, own_rows)], dst_ref=part_in,
         send_sem=part_sem.at[0], recv_sem=part_sem.at[1],
         device_id=(dp, mate), device_id_type=MESH,
     )
     part.start()
-    wave(1)
     meet(3, dp, mate)
 
     @pl.when(mid)
@@ -663,7 +664,7 @@
     width = out_grad.shape[1]
     own_rows = out_grad.shape[0]
     step_cols = hidden // 8
-    pieces = 4
+    pieces = 8
     dma = pltpu.SemaphoreType.DMA
     hbm = pl.BlockSpec(memory_space=pl.ANY)
     vmem = pl.BlockSpec(memory_space=pltpu.VMEM)

time: 167 us -> 167 us (level)
  no operation moved by 1% of the time
where the time goes in v7:
time: 167 us
  Pallas kernels  165 us (99%)
  local copies, waits for them, and re-layouts  1.67 us (1%)
    pallas_call x1, Pallas kernels, exchange(): pl.pallas_call(functools.partial(kernel, n_dp), out_shape=(jax.ShapeDtype...  165 us

profile of v7, /device:TPU:0, one launch (start us, length us, event | category | flops | bytes accessed | tf_op | source)
XLA Modules:
  0.0 167.0 jit_solution(8537347705832891324)
XLA Ops:
  0.6 164.7 %shard_map.50 = (bf16[256,512]{1,0:T(8,128)(2,1)S(1)}, f32[512,512]{1,0:T(8,128)S(1)}) custom-call(bf16[512,8192]{1,0:T(8,128)(2,1)} %pre.1, bf16[8192,512]{1,0:T(8,128)(2,1)} %w.1, bf16[256,512]{1,0:T(8,128)(2,1)} %og.1), custom_call_target="tpu_custom_call" | custom-call | tf_op jit(solution)/shard_map/pallas_call | solution.py:671
  165.3 0.7 copy.7
  166.0 1.0 copy.8
